TPU v7x, 128 devices: a whole 4x4x4 slice. The times are simulated.
128 devices in a mesh: branch: 4 (over z_lo, core), shard: 32 (over y, x, z_hi).
Axes of the slice: x: 4, y: 4, z: 4 (z_hi: 2, z_lo: 2; z = z_hi * 2 + z_lo), core: 2. Of those that a mesh axis runs over, the one named last changes fastest.
Arguments:
- attention_weights: bfloat16 [4, 2, 4096, 4096], P('branch', None, None, 'shard'), may hold values from -1.25 to 1.25
- ffn_weights: bfloat16 [4, 3, 4096, 11008], P('branch', None, 'shard'), may hold values from -0.3125 to 0.3125
- tokens: bfloat16 [2048, 4096], P(('branch', 'shard')), may hold values from -6 to 6
- routes: int32 [2048, 2], P(('branch', 'shard')), may hold values from 0 to 3, all different within a row; in each aligned block of 16 rows (0 to 15, 16 to 31, ...) at most 12 rows name the same one
- router: bfloat16 [4096, 4], replicated, may hold values from -0.09375 to 0.09375
Outputs:
- merged_attention: bfloat16 [2, 4096, 4096], P(None, 'branch', 'shard')
- expert_weights: bfloat16 [4, 3, 4096, 11008], P('branch', None, None, 'shard')
- mixed_output: bfloat16 [2048, 4096], P(('branch', 'shard'))
Inputs may be any that keep to these rules, and one draw needn't show every extreme that they name: `routes`: the 2 experts of a row differ. In each aligned block of 16 rows (the rows of one device) no expert is named by more than 12 rows, and in some blocks one expert is named by exactly 12 rows.
All inputs are finite; a program needn't handle non-finite values.
Results may differ from a plain program's by a relative error of at most 0.018.
Values may be sent and summed in bfloat16 or wider, within the bound.
A program may use at most 192 MiB of HBM per device.

v0:
```python
import jax
import jax.numpy as jnp
from jax import lax
from jax.sharding import Mesh
from jax.sharding import PartitionSpec as P

SHARD = ("shard_0", "shard_1", "shard_2")
BRANCH_SHARD = ("branch", "shard_0", "shard_1", "shard_2")


def own_rows(terms, axes):
    running = terms.astype(jnp.bfloat16)
    for axis in axes:
        running = lax.psum_scatter(running, axis, scatter_dimension=0, tiled=True)
    return running.astype(jnp.float32)


def slot_table(route_rows, experts_count, capacity):
    chosen = (route_rows[:, :, None] == jnp.arange(experts_count, dtype=jnp.int32)).astype(
        jnp.int32
    )
    flat_picks = chosen.reshape(-1, experts_count)
    before = jnp.cumsum(flat_picks, axis=0) - flat_picks
    position = jnp.sum(before * flat_picks, axis=1)
    slot_id = route_rows.reshape(-1) * capacity + position
    one_hot = (slot_id[:, None] == jnp.arange(experts_count * capacity, dtype=jnp.int32)).astype(
        jnp.float32
    )
    return jnp.sum(one_hot.reshape(route_rows.shape[0], route_rows.shape[1], -1), axis=1)


def local(attention_weights, ffn_weights, tokens, routes, router):
    branches = lax.axis_size("branch")
    expert_weights = lax.all_to_all(ffn_weights, SHARD, split_axis=3, concat_axis=2, tiled=True)
    gate_weight = expert_weights[0, 0]
    up_weight = expert_weights[0, 1]
    down_weight = expert_weights[0, 2]
    tok_count = tokens.shape[0]
    model_width = tokens.shape[1]
    capacity = 3 * tok_count // 4
    slot_map = slot_table(routes, branches, capacity)
    buffers = lax.dot_general(
        slot_map.astype(jnp.bfloat16),
        tokens,
        (((0,), (0,)), ((), ())),
        preferred_element_type=jnp.float32,
    )
    buffers = buffers.astype(jnp.bfloat16).reshape(branches, capacity, model_width)
    arrived = lax.all_to_all(buffers, "branch", split_axis=0, concat_axis=0, tiled=True)
    slot_rows = lax.all_gather(
        arrived.reshape(branches * capacity, model_width), SHARD, axis=0, tiled=True
    )
    gate_proj = jnp.dot(slot_rows, gate_weight, preferred_element_type=jnp.float32)
    up_proj = jnp.dot(slot_rows, up_weight, preferred_element_type=jnp.float32)
    hidden = (jax.nn.silu(gate_proj) * up_proj).astype(jnp.bfloat16)
    summed = own_rows(
        lax.dot_general(
            hidden, down_weight, (((1,), (1,)), ((), ())), preferred_element_type=jnp.float32
        ),
        SHARD,
    )
    outputs = summed.astype(jnp.bfloat16).reshape(branches, capacity, model_width)
    returned = lax.all_to_all(outputs, "branch", split_axis=0, concat_axis=0, tiled=True)
    gates_all = jax.nn.sigmoid(jnp.dot(tokens, router, preferred_element_type=jnp.float32))
    weighting = slot_map * jnp.repeat(gates_all, capacity, axis=1)
    mixed_output = jnp.dot(
        weighting, returned.reshape(branches * capacity, model_width).astype(jnp.float32)
    )
    mixed_output = mixed_output.astype(jnp.bfloat16)
    traded = lax.all_to_all(attention_weights, "branch", split_axis=2, concat_axis=0, tiled=True)
    summed_attention = jnp.sum(traded.astype(jnp.float32), axis=0)
    merged_attention = (summed_attention * (1.0 / branches)).astype(jnp.bfloat16)
    return (merged_attention, expert_weights, mixed_output)


def solution(mesh):
    torus = Mesh(
        mesh.devices.reshape(mesh.shape["branch"], 4, 4, 2),
        ("branch", "shard_0", "shard_1", "shard_2"),
    )
    in_specs = (
        P("branch", None, None, SHARD),
        P("branch", None, SHARD, None),
        P(BRANCH_SHARD, None),
        P(BRANCH_SHARD, None),
        P(),
    )
    out_specs = (P(None, "branch", SHARD), P("branch", None, None, SHARD), P(BRANCH_SHARD, None))
    return jax.shard_map(local, mesh=torus, in_specs=in_specs, out_specs=out_specs, check_vma=False)
```

profile of v0, /device:TPU:1, one launch (start us, length us, event | category | flops | bytes accessed | tf_op | source)
XLA Modules:
  0.0 518.2 jit_solution(2717877055317344785)
XLA Ops:
  7.2 0.8 copy.58
  8.2 0.2 select_reduce_fusion
  8.5 0.1 copy.59
  8.6 0.7 multiply_add_fusion
  9.4 0.3 convolution_convert_fusion.1
  9.7 0.1 reshape.45
  9.8 12.2 %all_to_all.37 = bf16[4,12,4096]{2,1,0:T(8,128)(2,1)S(1)} all-to-all(bf16[4,12,4096]{2,1,0:T(8,128)(2,1)S(1)} %reshape.45), channel_id=1, replica_groups=mesh['branch'=4,'shard_0'=4,'shard_1'=4,'shard_2'=2] {'branch'}, dimensions={0} | all-to-all | bytes 786432 | tf_op jit(solution)/shard_map/all_to_all | solution.py:49
  22.0 0.8 reshape.46
  22.9 17.6 %copy.55 = bf16[1,3,128,11008]{2,1,0,3:T(4,128)(2,1)} copy(bf16[1,3,128,11008]{3,2,1,0:T(8,128)(2,1)} %param.6) | data formatting | bytes 16908288 | tf_op args[1]
  40.5 145.7 %all_to_all.38 = bf16[1,3,128,11008]{2,1,0,3:T(4,128)(2,1)S(1)} all-to-all(bf16[1,3,128,11008]{2,1,0,3:T(4,128)(2,1)} %copy.55), channel_id=1, replica_groups=mesh['branch'=4,'shard_0'=4,'shard_1'=4,'shard_2'=2] {'shard_0','shard_1..., dimensions={3} | all-to-all | bytes 16908288 | tf_op jit(solution)/shard_map/all_to_all | solution.py:34
  186.2 5.0 copy.56
  191.3 9.2 %copy.67 = bf16[1,3,32,43,8,128]{5,4,2,3,1,0:T(8,128)(2,1)} copy(bf16[1,3,32,43,8,128]{5,4,3,2,1,0:T(8,128)(2,1)} %bitcast.32) | data formatting | bytes 16908288 | tf_op jit(solution)/shard_map/all_to_all | solution.py:34
  200.4 67.3 %all-gather.2.cloned.1.call-done = bf16[1536,4096]{1,0:T(8,128)(2,1)} async-done(((bf16[48,4096]{1,0:T(8,128)(2,1)}), bf16[1536,4096]{1,0:T(8,128)(2,1)}) %all-gather.2.cloned.1.call-update) | async-done | bytes 12582928 | tf_op jit(solution)/shard_map/all_gather | solution.py:50
  267.7 8.5 %fusion.1 = f32[1536,344]{0,1:T(8,128)S(1)} fusion(bf16[1536,4096]{1,0:T(8,128)(2,1)} %all-gather.2.cloned.1.call-done, bf16[1,3,4096,344]{2,3,1,0:T(8,128)(2,1)} %bitcast.33), kind=kOutput, calls=%fused_computation.10 | convolution fusion | flops 4328521728 | bytes 17514496 | tf_op jit(solution)/shard_map/dot_general | solution.py:53
  276.2 21.6 %convolution_convert_fusion = bf16[1536,4096]{1,0:T(8,128)(2,1)} fusion(bf16[1,3,4096,344]{2,3,1,0:T(8,128)(2,1)} %bitcast.34, bf16[1536,4096]{1,0:T(8,128)(2,1)} %all-gather.2.cloned.1.call-done, f32[1536,344]{0,1:T(8,128)S(1)} %fusion.1), kind=kOutput, calls=%fused_computation | convolution fusion | flops 8666505216 | bytes 32915456 | tf_op jit(solution)/shard_map/dot_general | solution.py:57
  297.8 113.0 %reduce-scatter.4.cloned.1.call-done = bf16[384,4096]{1,0:T(8,128)(2,1)} async-done(((bf16[1536,4096]{1,0:T(8,128)(2,1)}), bf16[384,4096]{1,0:T(8,128)(2,1)}) %reduce-scatter.4.cloned.1.call-update) | async-done | bytes 3145744 | tf_op jit(solution)/shard_map/reduce_scatter | solution.py:14
  410.8 0.2 reduce-scatter.8.cloned.1.call-start
  411.0 40.1 %reduce-scatter.6.cloned.1.call-done = bf16[96,4096]{1,0:T(8,128)(2,1)} async-done(((bf16[384,4096]{1,0:T(8,128)(2,1)}), bf16[96,4096]{1,0:T(8,128)(2,1)}) %reduce-scatter.6.cloned.1.call-update) | async-done | bytes 786448 | tf_op jit(solution)/shard_map/reduce_scatter | solution.py:14
  451.2 18.1 %copy.54 = bf16[1,2,4096,128]{3,1,0,2:T(2,128)(2,1)} copy(bf16[1,2,4096,128]{3,2,1,0:T(8,128)(2,1)S(1)} %copy-done.1) | data formatting | bytes 4194304 | tf_op args[0]
  469.3 4.4 all-to-all-start
  473.9 0.2 fusion.10
  474.0 0.1 copy.60
  474.1 0.1 broadcast_multiply_fusion
  474.2 0.5 reduce-scatter.8.cloned.1.call-done
  474.8 1.9 reshape.47
  476.6 21.8 %all-to-all-done = bf16[1,2,4096,128]{3,1,0,2:T(2,128)(2,1)S(1)} async-done(((bf16[1,2,4096,128]{3,1,0,2:T(2,128)(2,1)}), bf16[1,2,4096,128]{3,1,0,2:T(2,128)(2,1)S(1)}, u32[]{:S(2)}, u32[]{:S(2)}) %all-to-all-start) | async-done | bytes 2097184 | tf_op jit(solution)/shard_map/all_to_all | solution.py:70
  498.5 4.4 all-to-all-start.3
  502.9 2.1 convert_reduce_fusion
  505.0 0.5 multiply_convert_fusion
  505.5 0.9 copy.62
  506.3 4.4 all-to-all-done.3
  510.7 1.0 fusion
  (19 shorter events, 0.7 us)
Async XLA Ops:
  7.2 2.2 copy-start
  7.2 260.5 %all-gather.2.cloned.1.call-start = ((), (), s32[]{:S(2)}) async-start(), calls=%async_computation.7 | async-start | bytes 12976128 | tf_op jit(solution)/shard_map/all_gather | solution.py:50
  22.9 387.9 %reduce-scatter.4.cloned.1.call-start = ((), (), s32[]{:S(2)}) async-start(), calls=%async_computation.8 | async-start | bytes 15728640 | tf_op jit(solution)/shard_map/reduce_scatter | solution.py:14
  297.7 153.4 %copy-start.1 = (bf16[1,2,4096,128]{3,2,1,0:T(8,128)(2,1)S(1)}, bf16[1,2,4096,128]{3,2,1,0:T(8,128)(2,1)}, u32[]{:S(2)}) copy-start(bf16[1,2,4096,128]{3,2,1,0:T(8,128)(2,1)} %param.5) | copy-start | bytes 6291460
  297.8 153.4 %reduce-scatter.6.cloned.1.call-start = ((), (), s32[]{:S(2)}) async-start(), calls=%async_computation.9 | async-start | bytes 3932160 | tf_op jit(solution)/shard_map/reduce_scatter | solution.py:14
  410.8 64.0 %reduce-scatter.8.cloned.1.call-start = ((), (), s32[]{:S(2)}) async-start(), calls=%async_computation.10 | async-start | bytes 1179648 | tf_op jit(solution)/shard_map/reduce_scatter | solution.py:14
  469.3 4.5 copy-start.2
  469.3 29.1 %all-to-all-start = ((bf16[1,2,4096,128]{3,1,0,2:T(2,128)(2,1)}), bf16[1,2,4096,128]{3,1,0,2:T(2,128)(2,1)S(1)}, u32[]{:S(2)}, u32[]{:S(2)}) async-start(bf16[1,2,4096,128]{3,1,0,2:T(2,128)(2,1)} %copy.54), calls=%async_computation | async-start | bytes 4194304 | tf_op jit(solution)/shard_map/all_to_all | solution.py:70
  498.5 12.3 %all-to-all-start.3 = ((bf16[4,12,4096]{2,1,0:T(8,128)(2,1)}), bf16[4,12,4096]{2,1,0:T(8,128)(2,1)S(1)}, u32[]{:S(2)}, u32[]{:S(2)}) async-start(bf16[4,12,4096]{2,1,0:T(8,128)(2,1)} %reshape.47), calls=%async_computation.6 | async-start | bytes 1048576 | tf_op jit(solution)/shard_map/all_to_all | solution.py:63
Sparse Core Ops, SparseCore 0:
  23.0 244.6 all-gather.1
  297.9 112.8 reduce-scatter.3
  413.2 37.9 reduce-scatter.5
  453.4 21.3 reduce-scatter.7
where the time goes:
time: 519 us; the launch traced here: 518 us
  waiting for transfers between devices  247 us (48%)
  blocking collectives  158 us (30%)
  local copies, waits for them, and re-layouts  54.8 us (11%)
  matrix products  31.4 us (6%)
  between operations  13.9 us (3%)
  starting transfers between devices  9.18 us (2%)
    reduce_scatter x3, waiting for transfers between devices, own_rows(): running = lax.psum_scatter(running, axis, scatter_dimension=0, tiled=True)  154 us
    all_to_all x1, blocking collectives, local(): lax.all_to_all(ffn_weights, SHARD, split_axis=3, concat_axis=2, tiled=True)  146 us
    all_gather x1, waiting for transfers between devices, local(): lax.all_gather(arrived.reshape(branches * capacity, model_width), SHARD,...  67.3 us
    unnamed x10, local copies, waits for them, and re-layouts  37.4 us
    all_to_all x1, waiting for transfers between devices, local(): lax.all_to_all(attention_weights, 'branch', split_axis=2, concat_axis=0,...  21.8 us
    dot_general x1, matrix products, local(): lax.dot_general(hidden, down_weight, (((1,), (1,)), ((), ())), preferred_...  21.6 us
    all_to_all x2, local copies, waits for them, and re-layouts, local(): lax.all_to_all(ffn_weights, SHARD, split_axis=3, concat_axis=2, tiled=True)  14.2 us
    all_to_all x1, blocking collectives, local(): lax.all_to_all(buffers, 'branch', split_axis=0, concat_axis=0, tiled=True)  12.2 us
  transfers between devices with their start and end apart: 6, of which 6 were waited for; matrix products, arithmetic and copies ran while one was open for 11% of the time, Pallas kernels for 0%

commit v1 on v0

--- a/solution.py
+++ b/solution.py
@@ -3,6 +3,7 @@
 from jax import lax
 from jax.sharding import Mesh
 from jax.sharding import PartitionSpec as P
+from jax.lax import all_to_all, psum
 
 SHARD = ("shard_0", "shard_1", "shard_2")
 BRANCH_SHARD = ("branch", "shard_0", "shard_1", "shard_2")
@@ -31,7 +32,15 @@
 
 def local(attention_weights, ffn_weights, tokens, routes, router):
     branches = lax.axis_size("branch")
-    expert_weights = lax.all_to_all(ffn_weights, SHARD, split_axis=3, concat_axis=2, tiled=True)
+    expert_weights = jnp.concatenate(
+        all_to_all(
+            jnp.stack(jnp.split(ffn_weights, psum(1, axis_name=SHARD), axis=3)),
+            axis_name=SHARD,
+            split_axis=0,
+            concat_axis=0,
+        ),
+        axis=2,
+    )
     gate_weight = expert_weights[0, 0]
     up_weight = expert_weights[0, 1]
     down_weight = expert_weights[0, 2]

time: 519 us -> 496 us (0.956)
  local copies, waits for them, and re-layouts: 54.8 us -> 90.3 us
  waiting for transfers between devices: 247 us -> 216 us
  blocking collectives: 158 us -> 130 us
    all_gather x1, waiting for transfers between devices: 67.3 us -> 36.1 us  [local(): lax.all_gather(arrived.reshape(branches * capacity, model_width), SHARD,...]
    unnamed x10 -> x100, local copies, waits for them, and re-layouts: 37.4 us -> 66 us
    all_to_all x1, blocking collectives: 146 us -> 118 us  [local(): all_to_all(jnp.stack(jnp.split(ffn_weights, psum(1, axis_name=SHARD), axi...]
    all_to_all x2 -> x0, local copies, waits for them, and re-layouts: 14.2 us -> none  [local(): lax.all_to_all(ffn_weights, SHARD, split_axis=3, concat_axis=2, tiled=True)]
    split x0 -> x2, local copies, waits for them, and re-layouts: none -> 13 us  [local(): jnp.split(ffn_weights, psum(1, axis_name=SHARD), axis=3)]
    reshape x0 -> x1, local copies, waits for them, and re-layouts: none -> 8 us  [local(): jnp.concatenate(all_to_all(jnp.stack(jnp.split(ffn_weights, psum(1, axis_...]
  transfers between devices with their start and end apart: 6 -> 6, of which waited for: 6 -> 6; matrix products, arithmetic and copies ran while one was open for 11% -> 18% of each run, Pallas kernels for 0% -> 0%
where the time goes in v1:
time: 496 us; the launch traced here: 495 us
  waiting for transfers between devices  216 us (44%)
  blocking collectives  130 us (26%)
  local copies, waits for them, and re-layouts  90.3 us (18%)
  matrix products  31.4 us (6%)
  between operations  14.3 us (3%)
  starting transfers between devices  9.09 us (2%)
    reduce_scatter x3, waiting for transfers between devices, own_rows(): running = lax.psum_scatter(running, axis, scatter_dimension=0, tiled=True)  154 us
    all_to_all x1, blocking collectives, local(): all_to_all(jnp.stack(jnp.split(ffn_weights, psum(1, axis_name=SHARD), axi...  118 us
    unnamed x100, local copies, waits for them, and re-layouts  66 us
    all_gather x1, waiting for transfers between devices, local(): lax.all_gather(arrived.reshape(branches * capacity, model_width), SHARD,...  36.1 us
    all_to_all x1, waiting for transfers between devices, local(): lax.all_to_all(attention_weights, 'branch', split_axis=2, concat_axis=0,...  21.7 us
    dot_general x1, matrix products, local(): lax.dot_general(hidden, down_weight, (((1,), (1,)), ((), ())), preferred_...  21.6 us
    split x2, local copies, waits for them, and re-layouts, local(): jnp.split(ffn_weights, psum(1, axis_name=SHARD), axis=3)  13 us
    all_to_all x1, blocking collectives, local(): lax.all_to_all(buffers, 'branch', split_axis=0, concat_axis=0, tiled=True)  12.2 us
  transfers between devices with their start and end apart: 6, of which 6 were waited for; matrix products, arithmetic and copies ran while one was open for 18% of the time, Pallas kernels for 0%

profile of v1, /device:TPU:1, one launch (start us, length us, event | category | flops | bytes accessed | tf_op | source)
XLA Modules:
  0.0 495.3 jit_solution(4587957319680748992)
XLA Ops:
  9.8 12.2 %all_to_all.24 = bf16[4,12,4096]{2,1,0:T(8,128)(2,1)S(1)} all-to-all(bf16[4,12,4096]{2,1,0:T(8,128)(2,1)S(1)} %reshape.53), channel_id=1, replica_groups=mesh['branch'=4,'shard_0'=4,'shard_1'=4,'shard_2'=2] {'branch'}, dimensions={0} | all-to-all | bytes 786432 | tf_op jit(solution)/shard_map/all_to_all | solution.py:58
  22.9 5.3 %fusion.17 = (bf16[1,3,128,344]{3,2,1,0:T(8,128)(2,1)S(1)}, bf16[1,3,128,344]{3,2,1,0:T(8,128)(2,1)S(1)}, bf16[1,3,128,344]{3,2,1,0:T(8,128)(2,1)S(1)}, bf16[1,3...) fusion(bf16[1,3,128,11008]{3,2,1,0:T(8,128)(2,1)} %param.6), kind=kLoop, calls=%fused_computation.66 | loop fusion | bytes 6868992 | tf_op jit(solution)/shard_map/split | solution.py:37
  28.2 1.8 copy.214
  30.0 1.8 copy.215
  41.5 7.7 %fusion.16 = (bf16[1,3,128,344]{3,2,1,0:T(8,128)(2,1)S(1)}, bf16[1,3,128,344]{3,2,1,0:T(8,128)(2,1)S(1)}, bf16[1,3,128,344]{3,2,1,0:T(8,128)(2,1)S(1)}, bf16[1,3...) fusion(bf16[1,3,128,11008]{3,2,1,0:T(8,128)(2,1)} %param.6), kind=kLoop, calls=%fused_computation.65 | loop fusion | bytes 10039296 | tf_op jit(solution)/shard_map/split | solution.py:37
  49.2 1.8 copy.227
  51.0 1.8 copy.228
  52.8 1.8 copy.229
  54.6 1.8 copy.230
  56.5 1.8 copy.231
  58.3 1.8 copy.232
  60.1 1.8 copy.233
  62.0 1.8 copy.234
  69.5 1.1 bitcast_dynamic-update-slice_fusion.31
  70.6 1.0 bitcast_dynamic-update-slice_fusion.30
  72.6 1.0 bitcast_dynamic-update-slice_fusion.28
  73.6 1.0 bitcast_dynamic-update-slice_fusion.27
  74.6 1.0 bitcast_dynamic-update-slice_fusion.26
  82.6 118.2 %all_to_all.25 = bf16[32,1,3,128,344]{3,4,2,1,0:T(8,128)(2,1)} all-to-all(bf16[32,1,3,128,344]{3,4,2,1,0:T(8,128)(2,1)S(1)} %bitcast_dynamic-update-slice_fusion), channel_id=1, replica_groups=mesh['branch'=4,'shard_0'=4,'shard_1'=4,'shard_2'=2] {'shard_0','shard_1..., dimensions={0} | all-to-all | bytes 16908288 | tf_op jit(solution)/shard_map/all_to_all | solution.py:36
  200.8 8.0 %copy_bitcast_fusion = bf16[1,3,4096,344]{2,3,1,0:T(8,128)(2,1)} fusion(bf16[32,1,3,128,344]{3,4,2,1,0:T(8,128)(2,1)} %all_to_all.25), kind=kLoop, calls=%fused_computation.1 | loop fusion | bytes 16908288 | tf_op jit(solution)/shard_map/reshape | solution.py:35
  208.8 36.1 %all-gather.2.cloned.1.call-done = bf16[1536,4096]{1,0:T(8,128)(2,1)} async-done(((bf16[48,4096]{1,0:T(8,128)(2,1)}), bf16[1536,4096]{1,0:T(8,128)(2,1)}) %all-gather.2.cloned.1.call-update) | async-done | bytes 12582928 | tf_op jit(solution)/shard_map/all_gather | solution.py:59
  244.9 8.5 %fusion.1 = f32[1536,344]{0,1:T(8,128)S(1)} fusion(bf16[1536,4096]{1,0:T(8,128)(2,1)} %all-gather.2.cloned.1.call-done, bf16[1,3,4096,344]{2,3,1,0:T(8,128)(2,1)} %copy_bitcast_fusion), kind=kOutput, calls=%fused_computation.10 | convolution fusion | flops 4328521728 | bytes 17514496 | tf_op jit(solution)/shard_map/dot_general | solution.py:62
  253.4 21.6 %convolution_convert_fusion = bf16[1536,4096]{1,0:T(8,128)(2,1)} fusion(bf16[1,3,4096,344]{2,3,1,0:T(8,128)(2,1)} %copy_bitcast_fusion, bf16[1536,4096]{1,0:T(8,128)(2,1)} %all-gather.2.cloned.1.call-done, f32[1536,344]{0,1:T(8,128)S(1)} %fusion.1), kind=kOutput, calls=%fused_computation | convolution fusion | flops 8666505216 | bytes 32915456 | tf_op jit(solution)/shard_map/dot_general | solution.py:66
  275.0 113.0 %reduce-scatter.4.cloned.1.call-done = bf16[384,4096]{1,0:T(8,128)(2,1)} async-done(((bf16[1536,4096]{1,0:T(8,128)(2,1)}), bf16[384,4096]{1,0:T(8,128)(2,1)}) %reduce-scatter.4.cloned.1.call-update) | async-done | bytes 3145744 | tf_op jit(solution)/shard_map/reduce_scatter | solution.py:15
  388.3 40.1 %reduce-scatter.6.cloned.1.call-done = bf16[96,4096]{1,0:T(8,128)(2,1)} async-done(((bf16[384,4096]{1,0:T(8,128)(2,1)}), bf16[96,4096]{1,0:T(8,128)(2,1)}) %reduce-scatter.6.cloned.1.call-update) | async-done | bytes 786448 | tf_op jit(solution)/shard_map/reduce_scatter | solution.py:15
  428.4 18.1 %copy.175 = bf16[1,2,4096,128]{3,1,0,2:T(2,128)(2,1)} copy(bf16[1,2,4096,128]{3,2,1,0:T(8,128)(2,1)S(1)} %copy-done.1) | data formatting | bytes 4194304 | tf_op args[0]
  446.5 4.3 all-to-all-start
  452.0 1.9 reshape.55
  453.8 21.7 %all-to-all-done = bf16[1,2,4096,128]{3,1,0,2:T(2,128)(2,1)S(1)} async-done(((bf16[1,2,4096,128]{3,1,0,2:T(2,128)(2,1)}), bf16[1,2,4096,128]{3,1,0,2:T(2,128)(2,1)S(1)}, u32[]{:S(2)}, u32[]{:S(2)}) %all-to-all-start) | async-done | bytes 2097184 | tf_op jit(solution)/shard_map/all_to_all | solution.py:79
  475.5 4.4 all-to-all-start.3
  479.9 2.1 convert_reduce_fusion
  483.4 4.4 all-to-all-done.3
  (111 shorter events, 30.2 us)
Async XLA Ops:
  7.2 2.2 copy-start
  7.2 237.7 %all-gather.2.cloned.1.call-start = ((), (), s32[]{:S(2)}) async-start(), calls=%async_computation.7 | async-start | bytes 12976128 | tf_op jit(solution)/shard_map/all_gather | solution.py:59
  22.9 365.1 %reduce-scatter.4.cloned.1.call-start = ((), (), s32[]{:S(2)}) async-start(), calls=%async_computation.8 | async-start | bytes 15728640 | tf_op jit(solution)/shard_map/reduce_scatter | solution.py:15
  64.7 14.0 %copy-start.2 = (bf16[1,3,128,344]{2,3,1,0:T(8,128)(2,1)S(1)}, bf16[1,3,128,344]{2,3,1,0:T(8,128)(2,1)}, u32[]{:S(2)}) copy-start(bf16[1,3,128,344]{2,3,1,0:T(8,128)(2,1)} %copy.225) | copy-start | bytes 792580
  65.6 13.2 %copy-start.3 = (bf16[1,3,128,344]{2,3,1,0:T(8,128)(2,1)S(1)}, bf16[1,3,128,344]{2,3,1,0:T(8,128)(2,1)}, u32[]{:S(2)}) copy-start(bf16[1,3,128,344]{2,3,1,0:T(8,128)(2,1)} %copy.226) | copy-start | bytes 792580
  66.4 12.2 %copy-start.4 = (bf16[1,3,128,344]{2,3,1,0:T(8,128)(2,1)S(1)}, bf16[1,3,128,344]{2,3,1,0:T(8,128)(2,1)}, u32[]{:S(2)}) copy-start(bf16[1,3,128,344]{2,3,1,0:T(8,128)(2,1)} %copy.224) | copy-start | bytes 792580
  67.3 11.3 %copy-start.5 = (bf16[1,3,128,344]{2,3,1,0:T(8,128)(2,1)S(1)}, bf16[1,3,128,344]{2,3,1,0:T(8,128)(2,1)}, u32[]{:S(2)}) copy-start(bf16[1,3,128,344]{2,3,1,0:T(8,128)(2,1)} %copy.223) | copy-start | bytes 792580
  69.4 12.4 %copy-start.15 = (bf16[1,3,128,344]{2,3,1,0:T(8,128)(2,1)S(1)}, bf16[1,3,128,344]{2,3,1,0:T(8,128)(2,1)}, u32[]{:S(2)}) copy-start(bf16[1,3,128,344]{2,3,1,0:T(8,128)(2,1)} %copy.230) | copy-start | bytes 792580
  69.4 12.4 %copy-start.14 = (bf16[1,3,128,344]{2,3,1,0:T(8,128)(2,1)S(1)}, bf16[1,3,128,344]{2,3,1,0:T(8,128)(2,1)}, u32[]{:S(2)}) copy-start(bf16[1,3,128,344]{2,3,1,0:T(8,128)(2,1)} %copy.231) | copy-start | bytes 792580
  69.4 12.5 %copy-start.13 = (bf16[1,3,128,344]{2,3,1,0:T(8,128)(2,1)S(1)}, bf16[1,3,128,344]{2,3,1,0:T(8,128)(2,1)}, u32[]{:S(2)}) copy-start(bf16[1,3,128,344]{2,3,1,0:T(8,128)(2,1)} %copy.232) | copy-start | bytes 792580
  69.4 12.5 %copy-start.12 = (bf16[1,3,128,344]{2,3,1,0:T(8,128)(2,1)S(1)}, bf16[1,3,128,344]{2,3,1,0:T(8,128)(2,1)}, u32[]{:S(2)}) copy-start(bf16[1,3,128,344]{2,3,1,0:T(8,128)(2,1)} %copy.233) | copy-start | bytes 792580
  69.4 12.5 %copy-start.11 = (bf16[1,3,128,344]{2,3,1,0:T(8,128)(2,1)S(1)}, bf16[1,3,128,344]{2,3,1,0:T(8,128)(2,1)}, u32[]{:S(2)}) copy-start(bf16[1,3,128,344]{2,3,1,0:T(8,128)(2,1)} %copy.234) | copy-start | bytes 792580
  69.5 12.6 %copy-start.10 = (bf16[1,3,128,344]{2,3,1,0:T(8,128)(2,1)S(1)}, bf16[1,3,128,344]{2,3,1,0:T(8,128)(2,1)}, u32[]{:S(2)}) copy-start(bf16[1,3,128,344]{2,3,1,0:T(8,128)(2,1)} %copy.235) | copy-start | bytes 792580
  69.5 12.6 %copy-start.9 = (bf16[1,3,128,344]{2,3,1,0:T(8,128)(2,1)S(1)}, bf16[1,3,128,344]{2,3,1,0:T(8,128)(2,1)}, u32[]{:S(2)}) copy-start(bf16[1,3,128,344]{2,3,1,0:T(8,128)(2,1)} %copy.236) | copy-start | bytes 792580
  69.5 12.7 %copy-start.8 = (bf16[1,3,128,344]{2,3,1,0:T(8,128)(2,1)S(1)}, bf16[1,3,128,344]{2,3,1,0:T(8,128)(2,1)}, u32[]{:S(2)}) copy-start(bf16[1,3,128,344]{2,3,1,0:T(8,128)(2,1)} %copy.237) | copy-start | bytes 792580
  69.5 12.7 %copy-start.7 = (bf16[1,3,128,344]{2,3,1,0:T(8,128)(2,1)S(1)}, bf16[1,3,128,344]{2,3,1,0:T(8,128)(2,1)}, u32[]{:S(2)}) copy-start(bf16[1,3,128,344]{2,3,1,0:T(8,128)(2,1)} %copy.238) | copy-start | bytes 792580
  69.5 12.8 %copy-start.6 = (bf16[1,3,128,344]{2,3,1,0:T(8,128)(2,1)S(1)}, bf16[1,3,128,344]{2,3,1,0:T(8,128)(2,1)}, u32[]{:S(2)}) copy-start(bf16[1,3,128,344]{2,3,1,0:T(8,128)(2,1)} %copy.239) | copy-start | bytes 792580
  274.9 153.5 %copy-start.1 = (bf16[1,2,4096,128]{3,2,1,0:T(8,128)(2,1)S(1)}, bf16[1,2,4096,128]{3,2,1,0:T(8,128)(2,1)}, u32[]{:S(2)}) copy-start(bf16[1,2,4096,128]{3,2,1,0:T(8,128)(2,1)} %param.5) | copy-start | bytes 6291460
  274.9 176.0 %copy-start.16 = (bf16[4096,4]{0,1:T(4,128)(2,1)S(1)}, bf16[4096,4]{0,1:T(4,128)(2,1)}, u32[]{:S(2)}) copy-start(bf16[4096,4]{0,1:T(4,128)(2,1)} %param.9) | copy-start | bytes 98308
  275.0 153.4 %reduce-scatter.6.cloned.1.call-start = ((), (), s32[]{:S(2)}) async-start(), calls=%async_computation.9 | async-start | bytes 3932160 | tf_op jit(solution)/shard_map/reduce_scatter | solution.py:15
  388.0 64.0 %reduce-scatter.8.cloned.1.call-start = ((), (), s32[]{:S(2)}) async-start(), calls=%async_computation.10 | async-start | bytes 1179648 | tf_op jit(solution)/shard_map/reduce_scatter | solution.py:15
  446.5 29.0 %all-to-all-start = ((bf16[1,2,4096,128]{3,1,0,2:T(2,128)(2,1)}), bf16[1,2,4096,128]{3,1,0,2:T(2,128)(2,1)S(1)}, u32[]{:S(2)}, u32[]{:S(2)}) async-start(bf16[1,2,4096,128]{3,1,0,2:T(2,128)(2,1)} %copy.175), calls=%async_computation | async-start | bytes 4194304 | tf_op jit(solution)/shard_map/all_to_all | solution.py:79
  475.5 12.3 %all-to-all-start.3 = ((bf16[4,12,4096]{2,1,0:T(8,128)(2,1)}), bf16[4,12,4096]{2,1,0:T(8,128)(2,1)S(1)}, u32[]{:S(2)}, u32[]{:S(2)}) async-start(bf16[4,12,4096]{2,1,0:T(8,128)(2,1)} %reshape.55), calls=%async_computation.6 | async-start | bytes 1048576 | tf_op jit(solution)/shard_map/all_to_all | solution.py:72
Sparse Core Ops, SparseCore 0:
  23.0 221.8 all-gather.1
  275.1 112.8 reduce-scatter.3
  390.4 37.9 reduce-scatter.5
  430.6 21.3 reduce-scatter.7
